TPU v7x, 256 devices: a whole 4x4x8 slice. The times are simulated.
256 devices in a mesh: segment: 8 (over x, y_hi), dp: 32 (over y_lo, z, core).
Axes of the slice: x: 4, y: 4 (y_hi: 2, y_lo: 2; y = y_hi * 2 + y_lo), z: 8, core: 2. Of those that a mesh axis runs over, the one named last changes fastest.
Arguments:
- encoder_patch_input: bfloat16 [32, 1024, 1024], P('dp'), may hold values from -6 to 6
- encoder_norm_gains: float32 [8, 1024], P('segment'), may hold values from 0.5 to 1.5
- encoder_input_weight: bfloat16 [8, 1024, 2048], P('segment'), may hold values from -0.1875 to 0.1875
- encoder_output_weight: bfloat16 [8, 2048, 1024], P('segment'), may hold values from -0.125 to 0.125
- diffuser_hidden_states: bfloat16 [32, 1024, 2048], P('dp', 'segment'), may hold values from -6 to 6
- projector_first_weight: bfloat16 [2048, 2048], P('dp', 'segment'), may hold values from -0.125 to 0.125
- projector_second_weight: bfloat16 [2048, 1024], P(('segment', 'dp')), may hold values from -0.125 to 0.125
Outputs:
- grad_w1: float32 [2048, 2048], P('dp', 'segment')
- grad_w2: float32 [2048, 1024], P(('segment', 'dp'))
All inputs are finite; a program needn't handle non-finite values.
Results may differ from a plain program's by a relative error of at most 0.014.
Values may be sent and summed in bfloat16 or wider, within the bound.
A program may use at most 128 MiB of HBM per device.

v0:
```python
import jax
import jax.numpy as jnp
from jax import lax
from jax.sharding import PartitionSpec as P

norm_eps = 1e-06


def shifted(block, axis, distance):
    devices = range(lax.axis_size(axis))
    route = [(i - distance, i) for i in devices if i - distance in devices]
    return lax.ppermute(block, axis, route)


def from_root(block, axis, holder):
    block = jnp.where(lax.axis_index(axis) == holder, block, jnp.zeros_like(block))
    return lax.psum(block, axis)


def encoder_layer(hidden, scale_row, weight_in, weight_out):
    floats = hidden.astype(jnp.float32)
    normed = (
        floats * lax.rsqrt(jnp.mean(floats * floats, axis=-1, keepdims=True) + norm_eps) * scale_row
    )
    inner = jnp.dot(normed.astype(jnp.bfloat16), weight_in, preferred_element_type=jnp.float32)
    inner = jax.nn.gelu(inner, approximate=True).astype(jnp.bfloat16)
    return (floats + jnp.dot(inner, weight_out, preferred_element_type=jnp.float32)).astype(
        jnp.bfloat16
    )


def cosine_grad(projected, features):
    feat_f = features.astype(jnp.float32)
    squared = jnp.sum(projected * projected, axis=-1, keepdims=True) + norm_eps
    inv_proj = lax.rsqrt(squared)
    unit_feat = feat_f * lax.rsqrt(jnp.sum(feat_f * feat_f, axis=-1, keepdims=True) + norm_eps)
    cosine = jnp.sum(projected * unit_feat, axis=-1, keepdims=True) * inv_proj
    return (cosine * projected / squared - unit_feat * inv_proj).astype(jnp.bfloat16)


def silu_slope(preact):
    sigma = jax.nn.sigmoid(preact)
    return sigma * (1.0 + preact * (1.0 - sigma))


def contract_rows(left, right):
    return lax.dot_general(
        left, right, (((0,), (0,)), ((), ())), preferred_element_type=jnp.float32
    )


def on_device(
    encoder_patch_input,
    encoder_norm_gains,
    encoder_input_weight,
    encoder_output_weight,
    diffuser_hidden_states,
    projector_first_weight,
    projector_second_weight,
):
    segments = lax.axis_size("segment")
    segment_pos = lax.axis_index("segment")
    token_rows = diffuser_hidden_states.shape[1]
    source = encoder_patch_input[0]
    feat_width = source.shape[1]
    scale_row = encoder_norm_gains[0]
    weight_in = encoder_input_weight[0]
    weight_out = encoder_output_weight[0]

    def run_layer(entering):
        return encoder_layer(entering, scale_row, weight_in, weight_out)

    def pass_through(entering):
        return entering

    blank = jnp.zeros((token_rows, feat_width), jnp.bfloat16)
    inbound = blank
    finished = []
    for moment in range(2 * segments - 1):
        if moment < segments:
            inject = source[moment * token_rows : (moment + 1) * token_rows]
        else:
            inject = blank
        entering = jnp.where(segment_pos == 0, inject, inbound)
        active = jnp.logical_and(segment_pos <= moment, moment - segment_pos < segments)
        leaving = lax.cond(active, run_layer, pass_through, entering)
        if moment < 2 * segments - 2:
            inbound = shifted(leaving, "segment", 1)
        if moment >= segments - 1:
            finished.append(leaving)
    stacked = jnp.concatenate(finished, axis=0)
    everything = from_root(stacked, "segment", segments - 1)
    own_feats = lax.dynamic_slice_in_dim(everything, segment_pos * token_rows, token_rows, 0)
    first_block, second_block = (
        lax.all_gather(projector_first_weight, "dp", axis=0, tiled=True),
        lax.all_gather(projector_second_weight, "dp", axis=0, tiled=True),
    )
    hidden_combined = lax.all_gather(diffuser_hidden_states[0], "segment", axis=0, tiled=True)
    preact = jnp.dot(hidden_combined, first_block, preferred_element_type=jnp.float32)
    activated = jax.nn.silu(preact).astype(jnp.bfloat16)
    projected = lax.psum_scatter(
        jnp.dot(activated, second_block, preferred_element_type=jnp.float32),
        "segment",
        scatter_dimension=0,
        tiled=True,
    )
    grad_own = cosine_grad(projected, own_feats)
    grad_all = lax.all_gather(grad_own, "segment", axis=0, tiled=True)
    grad_second = contract_rows(activated, grad_all)
    back = lax.dot_general(
        grad_all, second_block, (((1,), (1,)), ((), ())), preferred_element_type=jnp.float32
    )
    grad_pre = (back * silu_slope(preact)).astype(jnp.bfloat16)
    grad_first = contract_rows(hidden_combined, grad_pre)
    first_rows, second_rows = (
        lax.psum_scatter(grad_first, "dp", scatter_dimension=0, tiled=True),
        lax.psum_scatter(grad_second, "dp", scatter_dimension=0, tiled=True),
    )
    return (first_rows, second_rows)


def solution(mesh):
    placed = (
        P("dp", None, None),
        P("segment", None),
        P("segment", None, None),
        P("segment", None, None),
        P("dp", "segment", None),
        P("dp", "segment"),
        P(("segment", "dp"), None),
    )
    return jax.shard_map(
        on_device,
        mesh=mesh,
        in_specs=placed,
        out_specs=(P("dp", "segment"), P(("segment", "dp"), None)),
        check_vma=False,
    )
```

profile of v0, /device:TPU:24, one launch (start us, length us, event | category | flops | bytes accessed | tf_op | source)
XLA Modules:
  0.0 759.5 jit_solution(12394751905636336380)
XLA Ops:
  13.2 9.9 %collective-permute-done = bf16[128,1024]{1,0:T(8,128)(2,1)S(1)} collective-permute-done((bf16[128,1024]{1,0:T(8,128)(2,1)S(1)}, bf16[128,1024]{1,0:T(8,128)(2,1)S(1)}, u32[]{:S(2)}, u32[]{:S(2)}) %collective-permute-start) | collective-permute-done | bytes 262176 | tf_op jit(solution)/shard_map/ppermute | solution.py:12
  23.2 5.3 conditional.16
  30.4 9.5 %collective-permute-done.1 = bf16[128,1024]{1,0:T(8,128)(2,1)S(1)} collective-permute-done((bf16[128,1024]{1,0:T(8,128)(2,1)S(1)}, bf16[128,1024]{1,0:T(8,128)(2,1)S(1)}, u32[]{:S(2)}, u32[]{:S(2)}) %collective-permute-start.1) | collective-permute-done | bytes 262176 | tf_op jit(solution)/shard_map/ppermute | solution.py:12
  40.0 5.3 conditional.17
  48.0 8.1 %collective-permute-done.2 = bf16[128,1024]{1,0:T(8,128)(2,1)S(1)} collective-permute-done((bf16[128,1024]{1,0:T(8,128)(2,1)S(1)}, bf16[128,1024]{1,0:T(8,128)(2,1)S(1)}, u32[]{:S(2)}, u32[]{:S(2)}) %collective-permute-start.2) | collective-permute-done | bytes 262176 | tf_op jit(solution)/shard_map/ppermute | solution.py:12
  56.1 5.3 conditional.18
  64.5 6.9 collective-permute-done.3
  71.4 5.3 conditional.19
  80.6 5.9 collective-permute-done.4
  86.5 5.3 conditional.20
  96.5 8.3 %collective-permute-done.5 = bf16[128,1024]{1,0:T(8,128)(2,1)S(1)} collective-permute-done((bf16[128,1024]{1,0:T(8,128)(2,1)S(1)}, bf16[128,1024]{1,0:T(8,128)(2,1)S(1)}, u32[]{:S(2)}, u32[]{:S(2)}) %collective-permute-start.5) | collective-permute-done | bytes 262176 | tf_op jit(solution)/shard_map/ppermute | solution.py:12
  104.9 5.5 conditional.21
  110.4 6.4 collective-permute-start.6
  125.9 6.8 collective-permute-start.7
  132.7 8.7 %collective-permute-done.7 = bf16[128,1024]{1,0:T(8,128)(2,1)S(1)} collective-permute-done((bf16[128,1024]{1,0:T(8,128)(2,1)S(1)}, bf16[128,1024]{1,0:T(8,128)(2,1)S(1)}, u32[]{:S(2)}, u32[]{:S(2)}) %collective-permute-start.7) | collective-permute-done | bytes 262176 | tf_op jit(solution)/shard_map/ppermute | solution.py:12
  141.4 5.3 conditional.23
  150.2 11.4 %collective-permute-done.8 = bf16[128,1024]{1,0:T(8,128)(2,1)S(1)} collective-permute-done((bf16[128,1024]{1,0:T(8,128)(2,1)S(1)}, bf16[128,1024]{1,0:T(8,128)(2,1)S(1)}, u32[]{:S(2)}, u32[]{:S(2)}) %collective-permute-start.8) | collective-permute-done | bytes 262176 | tf_op jit(solution)/shard_map/ppermute | solution.py:12
  161.6 6.0 collective-permute-start.9
  167.6 6.3 collective-permute-done.9
  173.9 6.4 collective-permute-start.10
  180.3 6.5 collective-permute-done.10
  186.9 6.8 collective-permute-start.11
  193.7 6.4 collective-permute-done.11
  201.3 6.9 collective-permute-start.12
  212.9 6.8 collective-permute-start.13
  225.2 36.8 %all_gather.14 = bf16[256,1024]{1,0:T(8,128)(2,1)S(1)} all-gather(bf16[8,1024]{1,0:T(8,128)(2,1)S(1)} %copy-done.2), channel_id=1, replica_groups=mesh['segment'=8,'dp'=32] {'dp'}, dimensions={0}, use_global_device_ids=true | all-gather | bytes 540672 | tf_op jit(solution)/shard_map/all_gather | solution.py:96
  268.6 89.6 %all-reduce.2.cloned.1.call-done = bf16[1024,1024]{1,0:T(8,128)(2,1)} async-done(((bf16[1024,1024]{1,0:T(8,128)(2,1)}), bf16[1024,1024]{1,0:T(8,128)(2,1)}) %all-reduce.2.cloned.1.call-update) | async-done | bytes 2097168 | tf_op jit(solution)/shard_map/psum | solution.py:17
  359.3 93.2 %reduce-scatter.6.cloned.1.call-done = f32[128,1024]{1,0:T(8,128)} async-done(((f32[1024,1024]{1,0:T(8,128)}), f32[128,1024]{1,0:T(8,128)}) %reduce-scatter.6.cloned.1.call-update) | async-done | bytes 524304 | tf_op jit(solution)/shard_map/reduce_scatter | solution.py:101
  456.0 59.0 %all-gather.7.cloned.1.call-done = bf16[1024,1024]{1,0:T(8,128)(2,1)} async-done(((bf16[128,1024]{1,0:T(8,128)(2,1)}), bf16[1024,1024]{1,0:T(8,128)(2,1)}) %all-gather.7.cloned.1.call-update) | async-done | bytes 2097168 | tf_op jit(solution)/shard_map/all_gather | solution.py:108
  518.4 6.1 fusion.469
  526.4 108.6 %reduce-scatter.8.cloned.1.call-done = f32[8,1024]{1,0:T(8,128)} async-done(((f32[256,1024]{1,0:T(8,128)}), f32[8,1024]{1,0:T(8,128)}) %reduce-scatter.8.cloned.1.call-update) | async-done | bytes 32784 | tf_op jit(solution)/shard_map/reduce_scatter | solution.py:117
  635.0 117.7 %reduce-scatter.10.cloned.1.call-done = f32[64,256]{1,0:T(8,128)} async-done(((f32[2048,256]{1,0:T(8,128)}), f32[64,256]{1,0:T(8,128)}) %reduce-scatter.10.cloned.1.call-update) | async-done | bytes 65552
  (105 shorter events, 104.9 us)
Async XLA Ops:
  7.2 254.8 %all-gather.5.cloned.1.call-start = ((), (), s32[]{:S(2)}) async-start(), calls=%async_computation.3 | async-start | bytes 1081344 | tf_op jit(solution)/shard_map/all_gather | solution.py:95
  7.9 254.1 %all-gather.9.cloned.1.call-start = ((), (), s32[]{:S(2)}) async-start(), calls=%async_computation.8 | async-start | bytes 4718592 | tf_op jit(solution)/shard_map/all_gather | solution.py:98
  8.9 14.2 %copy-start = (bf16[1,1024,1024]{2,1,0:T(8,128)(2,1)S(1)}, bf16[1,1024,1024]{2,1,0:T(8,128)(2,1)}, u32[]{:S(2)}) copy-start(bf16[1,1024,1024]{2,1,0:T(8,128)(2,1)} %param.37) | copy-start | bytes 6291460
  9.0 14.2 %collective-permute-start = (bf16[128,1024]{1,0:T(8,128)(2,1)S(1)}, bf16[128,1024]{1,0:T(8,128)(2,1)S(1)}, u32[]{:S(2)}, u32[]{:S(2)}) collective-permute-start(bf16[128,1024]{1,0:T(8,128)(2,1)S(1)} %get-tuple-element.251), channel_id=1, source_target_pairs={{0,32},{32,64},{64,96},{96,128},{128,160},{160,192},{192,224},{1,3... | collective-permute-start | bytes 786440 | tf_op jit(solution)/shard_map/ppermute | solution.py:12
  13.2 345.1 %all-reduce.2.cloned.1.call-start = ((), (), s32[]{:S(2)}) async-start(), calls=%async_computation.5 | async-start | bytes 4194304 | tf_op jit(solution)/shard_map/psum | solution.py:17
  28.5 11.5 %collective-permute-start.1 = (bf16[128,1024]{1,0:T(8,128)(2,1)S(1)}, bf16[128,1024]{1,0:T(8,128)(2,1)S(1)}, u32[]{:S(2)}, u32[]{:S(2)}) collective-permute-start(bf16[128,1024]{1,0:T(8,128)(2,1)S(1)} %get-tuple-element.252), channel_id=1, source_target_pairs={{0,32},{32,64},{64,96},{96,128},{128,160},{160,192},{192,224},{1,3... | collective-permute-start | bytes 786440 | tf_op jit(solution)/shard_map/ppermute | solution.py:12
  45.3 10.8 %collective-permute-start.2 = (bf16[128,1024]{1,0:T(8,128)(2,1)S(1)}, bf16[128,1024]{1,0:T(8,128)(2,1)S(1)}, u32[]{:S(2)}, u32[]{:S(2)}) collective-permute-start(bf16[128,1024]{1,0:T(8,128)(2,1)S(1)} %get-tuple-element.253), channel_id=1, source_target_pairs={{0,32},{32,64},{64,96},{96,128},{128,160},{160,192},{192,224},{1,3... | collective-permute-start | bytes 786440 | tf_op jit(solution)/shard_map/ppermute | solution.py:12
  61.4 10.0 %collective-permute-start.3 = (bf16[128,1024]{1,0:T(8,128)(2,1)S(1)}, bf16[128,1024]{1,0:T(8,128)(2,1)S(1)}, u32[]{:S(2)}, u32[]{:S(2)}) collective-permute-start(bf16[128,1024]{1,0:T(8,128)(2,1)S(1)} %get-tuple-element.254), channel_id=1, source_target_pairs={{0,32},{32,64},{64,96},{96,128},{128,160},{160,192},{192,224},{1,3... | collective-permute-start | bytes 786440 | tf_op jit(solution)/shard_map/ppermute | solution.py:12
  76.7 9.8 %collective-permute-start.4 = (bf16[128,1024]{1,0:T(8,128)(2,1)S(1)}, bf16[128,1024]{1,0:T(8,128)(2,1)S(1)}, u32[]{:S(2)}, u32[]{:S(2)}) collective-permute-start(bf16[128,1024]{1,0:T(8,128)(2,1)S(1)} %get-tuple-element.255), channel_id=1, source_target_pairs={{0,32},{32,64},{64,96},{96,128},{128,160},{160,192},{192,224},{1,3... | collective-permute-start | bytes 786440 | tf_op jit(solution)/shard_map/ppermute | solution.py:12
  91.8 13.0 %collective-permute-start.5 = (bf16[128,1024]{1,0:T(8,128)(2,1)S(1)}, bf16[128,1024]{1,0:T(8,128)(2,1)S(1)}, u32[]{:S(2)}, u32[]{:S(2)}) collective-permute-start(bf16[128,1024]{1,0:T(8,128)(2,1)S(1)} %get-tuple-element.256), channel_id=1, source_target_pairs={{0,32},{32,64},{64,96},{96,128},{128,160},{160,192},{192,224},{1,3... | collective-permute-start | bytes 786440 | tf_op jit(solution)/shard_map/ppermute | solution.py:12
  110.4 10.2 %collective-permute-start.6 = (bf16[128,1024]{1,0:T(8,128)(2,1)S(1)}, bf16[128,1024]{1,0:T(8,128)(2,1)S(1)}, u32[]{:S(2)}, u32[]{:S(2)}) collective-permute-start(bf16[128,1024]{1,0:T(8,128)(2,1)S(1)} %get-tuple-element.257), channel_id=1, source_target_pairs={{0,32},{32,64},{64,96},{96,128},{128,160},{160,192},{192,224},{1,3... | collective-permute-start | bytes 786440 | tf_op jit(solution)/shard_map/ppermute | solution.py:12
  125.9 15.5 %collective-permute-start.7 = (bf16[128,1024]{1,0:T(8,128)(2,1)S(1)}, bf16[128,1024]{1,0:T(8,128)(2,1)S(1)}, u32[]{:S(2)}, u32[]{:S(2)}) collective-permute-start(bf16[128,1024]{1,0:T(8,128)(2,1)S(1)} %get-tuple-element.258), channel_id=1, source_target_pairs={{0,32},{32,64},{64,96},{96,128},{128,160},{160,192},{192,224},{1,3... | collective-permute-start | bytes 786440 | tf_op jit(solution)/shard_map/ppermute | solution.py:12
  146.7 14.8 %collective-permute-start.8 = (bf16[128,1024]{1,0:T(8,128)(2,1)S(1)}, bf16[128,1024]{1,0:T(8,128)(2,1)S(1)}, u32[]{:S(2)}, u32[]{:S(2)}) collective-permute-start(bf16[128,1024]{1,0:T(8,128)(2,1)S(1)} %get-tuple-element.259), channel_id=1, source_target_pairs={{0,32},{32,64},{64,96},{96,128},{128,160},{160,192},{192,224},{1,3... | collective-permute-start | bytes 786440 | tf_op jit(solution)/shard_map/ppermute | solution.py:12
  161.6 12.3 %collective-permute-start.9 = (bf16[128,1024]{1,0:T(8,128)(2,1)S(1)}, bf16[128,1024]{1,0:T(8,128)(2,1)S(1)}, u32[]{:S(2)}, u32[]{:S(2)}) collective-permute-start(bf16[128,1024]{1,0:T(8,128)(2,1)S(1)} %get-tuple-element.260), channel_id=1, source_target_pairs={{0,32},{32,64},{64,96},{96,128},{128,160},{160,192},{192,224},{1,3... | collective-permute-start | bytes 786440 | tf_op jit(solution)/shard_map/ppermute | solution.py:12
  173.9 12.9 %collective-permute-start.10 = (bf16[128,1024]{1,0:T(8,128)(2,1)S(1)}, bf16[128,1024]{1,0:T(8,128)(2,1)S(1)}, u32[]{:S(2)}, u32[]{:S(2)}) collective-permute-start(bf16[128,1024]{1,0:T(8,128)(2,1)S(1)} %get-tuple-element.261), channel_id=1, source_target_pairs={{0,32},{32,64},{64,96},{96,128},{128,160},{160,192},{192,224},{1,3... | collective-permute-start | bytes 786440 | tf_op jit(solution)/shard_map/ppermute | solution.py:12
  186.9 13.3 %collective-permute-start.11 = (bf16[128,1024]{1,0:T(8,128)(2,1)S(1)}, bf16[128,1024]{1,0:T(8,128)(2,1)}, u32[]{:S(2)}, u32[]{:S(2)}) collective-permute-start(bf16[128,1024]{1,0:T(8,128)(2,1)S(1)} %get-tuple-element.262), channel_id=1, source_target_pairs={{0,32},{32,64},{64,96},{96,128},{128,160},{160,192},{192,224},{1,3... | collective-permute-start | bytes 786440 | tf_op jit(solution)/shard_map/ppermute | solution.py:12
  201.3 11.6 %collective-permute-start.12 = (bf16[128,1024]{1,0:T(8,128)(2,1)S(1)}, bf16[128,1024]{1,0:T(8,128)(2,1)S(1)}, u32[]{:S(2)}, u32[]{:S(2)}) collective-permute-start(bf16[128,1024]{1,0:T(8,128)(2,1)S(1)} %get-tuple-element.263), channel_id=1, source_target_pairs={{0,32},{32,64},{64,96},{96,128},{128,160},{160,192},{192,224},{1,3... | collective-permute-start | bytes 786440 | tf_op jit(solution)/shard_map/ppermute | solution.py:12
  212.9 10.7 %collective-permute-start.13 = (bf16[128,1024]{1,0:T(8,128)(2,1)S(1)}, bf16[128,1024]{1,0:T(8,128)(2,1)S(1)}, u32[]{:S(2)}, u32[]{:S(2)}) collective-permute-start(bf16[128,1024]{1,0:T(8,128)(2,1)S(1)} %get-tuple-element.264), channel_id=1, source_target_pairs={{0,32},{32,64},{64,96},{96,128},{128,160},{160,192},{192,224},{1,3... | collective-permute-start | bytes 786440 | tf_op jit(solution)/shard_map/ppermute | solution.py:12
  223.6 1.6 copy-start.2
  225.2 227.4 %reduce-scatter.6.cloned.1.call-start = ((), (), s32[]{:S(2)}) async-start(), calls=%async_computation.4 | async-start | bytes 4718592 | tf_op jit(solution)/shard_map/reduce_scatter | solution.py:101
  265.8 249.2 %copy-start.3 = (f32[1024,256]{1,0:T(8,128)}, f32[1024,256]{1,0:T(8,128)S(1)}, u32[]{:S(2)}) copy-start(f32[1024,256]{1,0:T(8,128)S(1)} %fusion.467) | copy-start | bytes 3145732
  268.6 246.4 %all-gather.7.cloned.1.call-start = ((), (), s32[]{:S(2)}) async-start(), calls=%async_computation.6 | async-start | bytes 2359296 | tf_op jit(solution)/shard_map/all_gather | solution.py:108
  455.9 179.1 %reduce-scatter.8.cloned.1.call-start = ((), (), s32[]{:S(2)}) async-start(), calls=%async_computation.7 | async-start | bytes 1081344 | tf_op jit(solution)/shard_map/reduce_scatter | solution.py:117
  518.3 234.3 %reduce-scatter.10.cloned.1.call-start = ((), (), s32[]{:S(2)}) async-start(), calls=%async_computation.9 | async-start | bytes 2162688
Sparse Core Ops, SparseCore 0:
  9.8 65.7 all-gather.4
  78.2 90.5 all-gather.8
  225.3 132.9 all-reduce.1
  362.3 90.2 reduce-scatter.5
  456.0 58.8 all-gather.6
  518.5 116.4 reduce-scatter.7
  638.2 114.3 reduce-scatter.9
where the time goes:
time: 761 us; the launch traced here: 759 us
  waiting for transfers between devices  569 us (75%)
  starting transfers between devices  70.2 us (9%)
  matrix products  56.8 us (7%)
  blocking collectives  36.8 us (5%)
  between operations  14.6 us (2%)
  other arithmetic  9.31 us (1%)
    unnamed x8, waiting for transfers between devices  118 us
    reduce_scatter x1, waiting for transfers between devices, on_device(): lax.psum_scatter(grad_second, 'dp', scatter_dimension=0, tiled=True)  109 us
    ppermute x14, waiting for transfers between devices, shifted(): return lax.ppermute(block, axis, route)  100 us
    reduce_scatter x1, waiting for transfers between devices, on_device(): lax.psum_scatter(jnp.dot(activated, second_block, preferred_element_type=...  93.2 us
    psum x1, waiting for transfers between devices, from_root(): return lax.psum(block, axis)  89.6 us
    ppermute x14, starting transfers between devices, shifted(): return lax.ppermute(block, axis, route)  69.9 us
    all_gather x1, waiting for transfers between devices, on_device(): grad_all = lax.all_gather(grad_own, 'segment', axis=0, tiled=True)  59 us
    dot_general x8, matrix products, encoder_layer(): jnp.dot(inner, weight_out, preferred_element_type=jnp.float32)  40.9 us
  transfers between devices with their start and end apart: 21, of which 19 were waited for; matrix products, arithmetic and copies ran while one was open for 8% of the time, Pallas kernels for 0%

commit v1 on v0

v1 whole, which is shorter than its diff:
```python
import functools

import jax
import jax.numpy as jnp
from jax import lax
from jax.experimental import pallas as pl
from jax.experimental.pallas import tpu as pltpu
from jax.sharding import PartitionSpec as P

EPS = 1e-06
GELU_C = 0.7978845608
F32 = jnp.float32
BF16 = jnp.bfloat16
CHUNKS = 8


def gelu(v):
    return 0.5 * v * (1.0 + jnp.tanh(GELU_C * (v + 0.044715 * (v * v * v))))


def mega(
    X,
    Z,
    x0_in,
    gain_in,
    wi_in,
    wo_in,
    hid_in,
    w1_in,
    w2_in,
    g1_out,
    g2_out,
    WI,
    WO,
    gains,
    x0,
    inbox,
    outbox,
    feat,
    hid,
    W1,
    W2,
    pre,
    act,
    pbuf,
    pown,
    precv,
    gall,
    gp,
    PB,
    crecv,
    S,
    urecv,
    usend,
    drecv,
    dsend,
    rsend,
    rown,
    yrecv,
    lsem,
    gsem,
    ws,
    wr,
    hs,
    hr,
    ags,
    agr,
    pxs,
    pxr,
    pis,
    pir,
    fs,
    fr,
    pps,
    ppr,
    ggs,
    ggr,
    ccs,
    ccr,
    us,
    ur,
    ds_,
    dr,
    ys,
    yr,
):
    seg = lax.axis_index("segment")
    dp = lax.axis_index("dp")
    x = seg // 2
    yh = seg % 2
    yl = dp // (2 * Z)
    z = (dp // 2) % Z
    c = dp % 2
    y = yh * 2 + yl
    zp = z % 2
    T, D = hid.shape[1], x0.shape[2]

    def dev(xx=x, yy=y, zz=z, cc=c):
        return {
            "segment": xx * 2 + yy // 2,
            "dp": (yy % 2) * (2 * Z) + zz * 2 + cc,
        }

    def push(src, dst, ssem, rsem, to):
        pltpu.make_async_remote_copy(
            src_ref=src,
            dst_ref=dst,
            send_sem=ssem,
            recv_sem=rsem,
            device_id=to,
            device_id_type=pl.DeviceIdType.MESH,
        ).start()

    def wait(ref, sem):
        pltpu.make_async_copy(ref, ref, sem).wait()

    def loop(lo, hi, body):
        def step(i, carry):
            body(i)
            return carry

        lax.fori_loop(lo, hi, step, 0)

    partner = dev(cc=1 - c)
    cut = dev(yy=3 - y)
    mate = dev(yy=yh * 2 + (1 - yl))
    up = dev(zz=(z + 1) % Z)
    down = dev(zz=(z + Z - 1) % Z)

    local = [
        pltpu.make_async_copy(wi_in, WI.at[yh], lsem.at[0]),
        pltpu.make_async_copy(wo_in, WO.at[yh], lsem.at[1]),
        pltpu.make_async_copy(hid_in, hid.at[x], lsem.at[2]),
        pltpu.make_async_copy(gain_in, gains.at[yh], lsem.at[3]),
        pltpu.make_async_copy(
            w1_in, W1.at[yl * Z + z, c, :, pl.ds(pl.multiple_of(yh * 256, 256), 256)], lsem.at[4]
        ),
        pltpu.make_async_copy(w2_in, W2.at[yh, yl * Z + z, c], lsem.at[5]),
    ] + [
        pltpu.make_async_copy(
            x0_in.at[pl.ds(pl.multiple_of((2 * m + yh) * T, T), T), :], x0.at[m], lsem.at[6 + m]
        )
        for m in range(X)
    ]
    for copy in local:
        copy.start()

    barrier = pltpu.get_barrier_semaphore()

    def greet(to):
        pl.semaphore_signal(barrier, inc=1, device_id=to, device_id_type=pl.DeviceIdType.MESH)

    greet(partner)
    for i in range(1, X):
        greet(dev(xx=(x + i) % X))
    loop(1, 4 * Z, lambda k: greet(dev(yy=(y + k // Z) % 4, zz=(z + k % Z) % Z)))
    pl.semaphore_wait(barrier, 1 + (X - 1) + (4 * Z - 1))

    for i in range(1, X):
        push(hid_in, hid.at[x], hs.at[i], hr.at[x], dev(xx=(x + i) % X))

    push(gain_in, gains.at[yh], gsem.at[0], gsem.at[1], cut)
    other = 1 - yh

    def part(ref, slot, piece, k):
        rows = ref.shape[1] // 8
        step = rows // CHUNKS
        if slot is None:
            return ref.at[pl.ds(pl.multiple_of(piece * rows + k * step, step), step), :]
        return ref.at[slot, pl.ds(pl.multiple_of(piece * rows + k * step, step), step), :]

    def native(ref, like, piece, k):
        rows = like.shape[1] // 8
        step = rows // CHUNKS
        return ref.at[pl.ds(pl.multiple_of(piece * rows + k * step, step), step), :]

    quarter_cut = 2 * (2 * zp + (1 - yl)) + c
    quarter = [
        2 * (2 * zp + yl) + c,
        2 * (2 * zp + (1 - yl)) + c,
        2 * (2 * (1 - zp) + yl) + c,
        2 * (2 * (1 - zp) + (1 - yl)) + c,
    ]
    pair = [(0, WI, wi_in), (1, WO, wo_in)]

    def first(k):
        for w, buf, src in pair:
            push(
                native(src, buf, quarter_cut, k),
                part(buf, yh, quarter_cut, k),
                ws.at[w, 0, k],
                wr.at[w, 0, k],
                cut,
            )

    loop(0, CHUNKS, first)

    def relay(q, recv_kind, k, targets):
        for w, buf, _ in pair:
            got = part(buf, other, quarter[q], k)
            wait(got, wr.at[w, recv_kind, k])
            for kind, to in targets:
                push(got, got, ws.at[w, kind, k], wr.at[w, kind, k], to)

    def exchange(t):
        @pl.when(t < CHUNKS)
        def _():
            relay(0, 0, t, [(1, mate), (2, up), (3, partner)])

        @pl.when(jnp.logical_and(t >= 1, t < CHUNKS + 1))
        def _():
            relay(1, 1, t - 1, [(4, down), (5, partner)])

        @pl.when(jnp.logical_and(t >= 2, t < CHUNKS + 2))
        def _():
            relay(2, 2, t - 2, [(6, partner)])

        @pl.when(t >= 3)
        def _():
            relay(3, 4, t - 3, [(7, partner)])

    loop(0, CHUNKS + 3, exchange)

    mine = y * Z + z

    def gather(k):
        to = dev(yy=(y + k // Z) % 4, zz=(z + k % Z) % Z)
        push(
            w1_in,
            W1.at[yl * Z + z, c, :, pl.ds(pl.multiple_of(yh * 256, 256), 256)],
            ags.at[0, k],
            agr.at[0, mine],
            to,
        )
        push(w2_in, W2.at[yh, yl * Z + z, c], ags.at[1, k], agr.at[1, mine], to)

    loop(1, 4 * Z, gather)

    def partner_share(k):
        for q, kind in enumerate((3, 5, 6, 7)):
            for w, buf, _ in pair:
                theirs = part(buf, other, quarter[q] + (1 - 2 * c), k)
                wait(theirs, wr.at[w, kind, k])

    loop(0, CHUNKS, partner_share)
    wait(gains.at[other], gsem.at[1])
    for copy in local:
        copy.wait()

    def encode(m):
        @pl.when(x > 0)
        def _():
            wait(inbox.at[m], pir.at[m])

        @pl.when(x == 0)
        def _():
            inbox[m] = x0[m]

        def layer(j):
            h = inbox[m].astype(F32)
            scale = lax.rsqrt(jnp.mean(h * h, axis=-1, keepdims=True) + EPS)
            n = (h * scale * gains[j]).astype(BF16)
            u = jnp.dot(n, WI[j], preferred_element_type=F32)
            u = gelu(u).astype(BF16)
            r = (h + jnp.dot(u, WO[j], preferred_element_type=F32)).astype(BF16)

            @pl.when(j == 0)
            def _():
                inbox[m] = r

            @pl.when(j == 1)
            def _():
                outbox[m] = r

        loop(0, 2, layer)

        @pl.when(x < X - 1)
        def _():
            push(outbox.at[m], inbox.at[m], pis.at[m], pir.at[m], dev(xx=x + 1))

        @pl.when(jnp.logical_and(x == X - 1, m < X - 1))
        def _():
            push(outbox.at[m], feat, fs.at[m], fr, dev(xx=m))

    def project():
        def arrived(k):
            yy, zz = k // Z, k % Z
            row = (yy % 2) * Z + zz
            col = pl.multiple_of((yy // 2) * 256, 256)

            @pl.when(k != mine)
            def _():
                wait(W1.at[row, c, :, pl.ds(col, 256)], agr.at[0, k])
                wait(W2.at[yy // 2, row, c], agr.at[1, k])

        loop(0, 4 * Z, arrived)
        push(W1.at[:, c], W1.at[:, c], pxs.at[0], pxr.at[0], partner)
        for h in range(2):
            push(W2.at[h, :, c], W2.at[h, :, c], pxs.at[1 + h], pxr.at[1 + h], partner)
        for i in range(1, X):
            xx = (x + i) % X
            wait(hid.at[xx], hr.at[xx])
        wait(W1.at[:, 1 - c], pxr.at[0])
        for h in range(2):
            wait(W2.at[h, :, 1 - c], pxr.at[1 + h])

        def block(j):
            w1 = W1[...].reshape(W1.shape[0] * 2 * W1.shape[2], W1.shape[3])
            w2 = W2[...].reshape(W2.shape[0] * W2.shape[1] * 2 * W2.shape[3], W2.shape[4])
            v = jnp.dot(hid[j], w1, preferred_element_type=F32)
            pre[j] = v
            a = (v / (1.0 + jnp.exp(-v))).astype(BF16)
            act[j] = a
            p = jnp.dot(a, w2, preferred_element_type=F32)

            @pl.when(j == x)
            def _():
                pown[...] = p

            @pl.when(j != x)
            def _():
                pbuf[j] = p.astype(BF16)
                push(pbuf.at[j], precv.at[x], pps.at[j], ppr.at[x], dev(xx=j))

        loop(0, X, block)

    def order(phase):
        @pl.when((phase == 0) == (x == X - 1))
        def _():
            project()

        @pl.when(phase == 0)
        def _():
            loop(0, X, encode)

    loop(0, 2, order)

    total = pown[...]
    for i in range(1, X):
        xx = (x + i) % X
        wait(precv.at[xx], ppr.at[xx])
        total = total + precv[xx].astype(F32)

    @pl.when(x < X - 1)
    def _():
        wait(feat, fr)

    @pl.when(x == X - 1)
    def _():
        feat[...] = outbox[X - 1]

    f = feat[...].astype(F32)
    squared = jnp.sum(total * total, axis=-1, keepdims=True) + EPS
    inv = lax.rsqrt(squared)
    unit = f * lax.rsqrt(jnp.sum(f * f, axis=-1, keepdims=True) + EPS)
    cosine = jnp.sum(total * unit, axis=-1, keepdims=True) * inv
    gall[x] = (cosine * total / squared - unit * inv).astype(BF16)
    for i in range(1, X):
        push(gall.at[x], gall.at[x], ggs.at[i], ggr.at[x], dev(xx=(x + i) % X))

    def back(i):
        j = (x + i) % X

        @pl.when(i > 0)
        def _():
            wait(gall.at[j], ggr.at[j])

        w2 = W2[...].reshape(W2.shape[0] * W2.shape[1] * 2 * W2.shape[3], W2.shape[4])
        b = lax.dot_general(gall[j], w2, (((1,), (1,)), ((), ())), preferred_element_type=F32)
        v = pre[j]
        s = 1.0 / (1.0 + jnp.exp(-v))
        gp[j] = (b * (s * (1.0 + v * (1.0 - s)))).astype(BF16)

    loop(0, X, back)

    tokens = X * T
    rows_dims = (((0,), (0,)), ((), ()))
    g2 = lax.dot_general(
        act[...].reshape(tokens, act.shape[2]),
        gall[...].reshape(tokens, D),
        rows_dims,
        preferred_element_type=F32,
    ).reshape(2, 2, Z, 2, 8, D)
    gpv = gp[...].reshape(tokens, gp.shape[2])
    span = Z // 2 * 2 * 64
    for q in range(4):
        g1 = lax.dot_general(
            hid[:, :, q * span : (q + 1) * span].reshape(tokens, span),
            gpv,
            rows_dims,
            preferred_element_type=F32,
        ).reshape(Z // 2, 2, 64, 512)
        yl2, z2 = q // 2, (q % 2) * (Z // 2)
        for cc in range(2):
            for yh2 in range(2):
                PB[cc, yh2 * 2 + yl2, z2 : z2 + Z // 2, 0:64, :] = g1[
                    :, cc, :, yh2 * 256 : yh2 * 256 + 256
                ].astype(BF16)
    for cc in range(2):
        for yy in range(4):
            for zz in range(Z):
                blk = g2[yy // 2, yy % 2, zz, cc]
                PB[cc, yy, zz, 64:96, :] = jnp.concatenate(
                    [blk[:, k * 256 : k * 256 + 256] for k in range(4)], axis=0
                ).astype(BF16)

    for yy in range(4):
        push(PB.at[1 - c, yy], crecv.at[yy], ccs.at[yy], ccr.at[yy], partner)

    half = Z // 2

    def cores(yy):
        wait(crecv.at[yy], ccr.at[yy])
        S[yy] = (PB[c, yy].astype(F32) + crecv[yy].astype(F32)).astype(BF16)
        push(S.at[yy, (z + half) % Z], urecv.at[0, yy], us.at[0, yy], ur.at[0, yy], up)
        push(S.at[yy, (z + half + 1) % Z], drecv.at[0, yy], ds_.at[0, yy], dr.at[0, yy], down)

    loop(0, 4, cores)

    def ring(t):
        for yy in range(4):
            wait(urecv.at[t, yy], ur.at[t, yy])
            usend[t, yy] = (
                urecv[t, yy].astype(F32) + S[yy, (z + half - 1 - t) % Z].astype(F32)
            ).astype(BF16)
            push(usend.at[t, yy], urecv.at[t + 1, yy], us.at[t + 1, yy], ur.at[t + 1, yy], up)

            @pl.when(t < half - 2)
            def _():
                wait(drecv.at[t, yy], dr.at[t, yy])
                dsend[t, yy] = (
                    drecv[t, yy].astype(F32) + S[yy, (z + half + 2 + t) % Z].astype(F32)
                ).astype(BF16)
                push(
                    dsend.at[t, yy], drecv.at[t + 1, yy], ds_.at[t + 1, yy], dr.at[t + 1, yy], down
                )

    loop(0, half - 1, ring)

    def rows(yy):
        wait(urecv.at[half - 1, yy], ur.at[half - 1, yy])
        wait(drecv.at[half - 2, yy], dr.at[half - 2, yy])
        r = (
            S[yy, z].astype(F32)
            + urecv[half - 1, yy].astype(F32)
            + drecv[half - 2, yy].astype(F32)
        )

        @pl.when(yy == y)
        def _():
            rown[...] = r

        @pl.when(yy != y)
        def _():
            rsend[yy] = r.astype(BF16)
            push(rsend.at[yy], yrecv.at[y], ys.at[yy], yr.at[y], dev(yy=yy))

    loop(0, 4, rows)
    r = rown[...]
    for i in range(1, 4):
        yy = (y + i) % 4
        wait(yrecv.at[yy], yr.at[yy])
        r = r + yrecv[yy].astype(F32)
    g1_out[...] = r[0:64]
    for k in range(4):
        g2_out[:, k * 256 : k * 256 + 256] = r[64 + 8 * k : 72 + 8 * k]

    for i in range(1, X):
        wait(hid.at[x], hs.at[i])
        wait(gall.at[x], ggs.at[i])
    wait(gains.at[yh], gsem.at[0])

    def sent_weights(k):
        for w, buf, _ in pair:
            for kind in range(8):
                wait(part(buf, 0, 0, k), ws.at[w, kind, k])

    loop(0, CHUNKS, sent_weights)

    def sent_gather(k):
        wait(w1_in, ags.at[0, k])
        wait(w2_in, ags.at[1, k])

    loop(1, 4 * Z, sent_gather)
    wait(W1.at[:, c], pxs.at[0])
    for h in range(2):
        wait(W2.at[h, :, c], pxs.at[1 + h])

    def sent_lines(m):
        @pl.when(x < X - 1)
        def _():
            wait(outbox.at[m], pis.at[m])

        @pl.when(jnp.logical_and(x == X - 1, m < X - 1))
        def _():
            wait(outbox.at[m], fs.at[m])

        @pl.when(m != x)
        def _():
            wait(pbuf.at[m], pps.at[m])

    loop(0, X, sent_lines)

    def sent_sums(yy):
        wait(crecv.at[yy], ccs.at[yy])
        for t in range(half):
            wait(urecv.at[0, yy], us.at[t, yy])
        for t in range(half - 1):
            wait(drecv.at[0, yy], ds_.at[t, yy])

        @pl.when(yy != y)
        def _():
            wait(rsend.at[yy], ys.at[yy])

    loop(0, 4, sent_sums)


def solution(mesh):
    X = mesh.shape["segment"] // 2
    Z = mesh.shape["dp"] // 4

    def on_device(x0, gain, wi, wo, hid, w1, w2):
        x0, wi, wo, hid = x0[0], wi[0], wo[0], hid[0]
        T, W = hid.shape
        N, D = x0.shape
        E = wi.shape[1]
        H = 2 * w1.shape[1]
        half = Z // 2
        B = (96, 256)
        vm = lambda shape, dtype=BF16: pltpu.VMEM(shape, dtype)
        dma = lambda *shape: pltpu.SemaphoreType.DMA(shape)
        scratch = [
            vm((2, D, E)),
            vm((2, E, D)),
            vm((2, 1, D), F32),
            vm((X, T, D)),
            vm((X, T, D)),
            vm((X, T, D)),
            vm((T, D)),
            vm((X, T, W)),
            vm((2 * Z, 2, 64, H)),
            vm((2, 2 * Z, 2, 8, D)),
            vm((X, T, H), F32),
            vm((X, T, H)),
            vm((X, T, D)),
            vm((T, D), F32),
            vm((X, T, D)),
            vm((X, T, D)),
            vm((X, T, H)),
            vm((2, 4, Z) + B),
            vm((4, Z) + B),
            vm((4, Z) + B),
            vm((half, 4) + B),
            vm((half - 1, 4) + B),
            vm((half - 1, 4) + B),
            vm((half - 2, 4) + B),
            vm((4,) + B),
            vm(B, F32),
            vm((4,) + B),
            dma(6 + X),
            dma(2),
            dma(2, 8, CHUNKS),
            dma(2, 8, CHUNKS),
            dma(X),
            dma(X),
            dma(2, 4 * Z),
            dma(2, 4 * Z),
            dma(3),
            dma(3),
            dma(X),
            dma(X),
            dma(X),
            pltpu.SemaphoreType.DMA,
            dma(X),
            dma(X),
            dma(X),
            dma(X),
            dma(4),
            dma(4),
            dma(half, 4),
            dma(half, 4),
            dma(half - 1, 4),
            dma(half - 1, 4),
            dma(4),
            dma(4),
        ]
        any_ = pl.BlockSpec(memory_space=pl.ANY)
        vmem = pl.BlockSpec(memory_space=pltpu.VMEM)
        return pl.pallas_call(
            functools.partial(mega, X, Z),
            out_shape=(
                jax.ShapeDtypeStruct((64, 256), F32),
                jax.ShapeDtypeStruct((8, D), F32),
            ),
            in_specs=[any_, vmem, any_, any_, any_, vmem, vmem],
            out_specs=(vmem, vmem),
            scratch_shapes=scratch,
            compiler_params=pltpu.CompilerParams(
                collective_id=0, has_side_effects=True, vmem_limit_bytes=62 << 20
            ),
        )(x0, gain, wi, wo, hid, w1, w2)

    placed = (
        P("dp", None, None),
        P("segment", None),
        P("segment", None, None),
        P("segment", None, None),
        P("dp", "segment", None),
        P("dp", "segment"),
        P(("segment", "dp"), None),
    )
    return jax.shard_map(
        on_device,
        mesh=mesh,
        in_specs=placed,
        out_specs=(P("dp", "segment"), P(("segment", "dp"), None)),
        check_vma=False,
    )
```

time: 761 us -> 159 us (0.21)
  waiting for transfers between devices: 569 us -> 0 us
  Pallas kernels: 0 us -> 155 us
  starting transfers between devices: 70.2 us -> 0 us
  matrix products: 56.8 us -> 0 us
  blocking collectives: 36.8 us -> 0 us
  between operations: 14.6 us -> 0.64 us
  other arithmetic: 9.31 us -> 0 us
    reduce_scatter x2 -> x0, waiting for transfers between devices: 202 us -> none  [the longest x1 109 us: on_device(): lax.psum_scatter(grad_second, 'dp', scatter_dimension=0, tiled=True)]
    pallas_call x0 -> x1, Pallas kernels: none -> 155 us  [on_device(): pl.pallas_call(functools.partial(mega, X, Z), out_shape=(jax.ShapeDtypeSt...]
    unnamed x8 -> x0, waiting for transfers between devices: 118 us -> none
    ppermute x14 -> x0, waiting for transfers between devices: 100 us -> none  [shifted(): return lax.ppermute(block, axis, route)]
    psum x1 -> x0, waiting for transfers between devices: 89.6 us -> none  [from_root(): return lax.psum(block, axis)]
    ppermute x14 -> x0, starting transfers between devices: 69.9 us -> none  [shifted(): return lax.ppermute(block, axis, route)]
    all_gather x3 -> x0, waiting for transfers between devices: 59 us -> none  [the longest x1 59 us: on_device(): grad_all = lax.all_gather(grad_own, 'segment', axis=0, tiled=True)]
    dot_general x12 -> x0, matrix products: 56.8 us -> none  [the longest x8 40.9 us: encoder_layer(): jnp.dot(inner, weight_out, preferred_element_type=jnp.float32)]
  transfers between devices with their start and end apart: 21 -> 0, of which waited for: 19 -> 0; matrix products, arithmetic and copies ran while one was open for 8% -> 0% of each run, Pallas kernels for 0% -> 0%
where the time goes in v1:
time: 159 us
  Pallas kernels  155 us (97%)
  local copies, waits for them, and re-layouts  2.85 us (2%)
    pallas_call x1, Pallas kernels, on_device(): pl.pallas_call(functools.partial(mega, X, Z), out_shape=(jax.ShapeDtypeSt...  155 us

profile of v1, /device:TPU:24, one launch (start us, length us, event | category | flops | bytes accessed | tf_op | source)
XLA Modules:
  0.0 158.8 jit_solution(11730687076454722516)
XLA Ops:
  0.6 155.3 %shard_map.86 = (f32[64,256]{1,0:T(8,128)}, f32[8,1024]{1,0:T(8,128)}) custom-call(bf16[1024,1024]{1,0:T(8,128)(2,1)} %bitcast.6, f32[1,1024]{1,0:T(1,128)} %gain_in.1, bf16[1024,2048]{1,0:T(8,128)(2,1)} %bitcast.4, bf16[2048,1024]{1,0:T(8,128)(2,1)} %bitcast.5, bf16[128,2048]{1,0:T(8,128)(2,1)} %bitcast.7, bf16[64,256]{1,0:T(8,128)(2,1)} %w1_in.1, ...), custom_call_target="tpu_custom_call" | custom-call | tf_op jit(solution)/shard_map/pallas_call | solution.py:589
  155.9 1.5 copy.11
  157.4 1.4 copy.12

commit v2 on v1

--- a/solution.py
+++ b/solution.py
@@ -193,6 +193,50 @@
                 cut,
             )
 
+    mine = y * Z + z
+    half = Z // 2
+    turn = 1 - 2 * c
+    ahead = dev(zz=(z + Z + turn) % Z)
+    behind = dev(zz=(z + Z - turn) % Z)
+
+    def slab(yy, zz):
+        row = (yy % 2) * Z + zz
+        col = pl.multiple_of((yy // 2) * 256, 256)
+        return W1.at[row, c, :, pl.ds(col, 256)], W2.at[yy // 2, row, c]
+
+    for i in range(1, 4):
+        for w, (src, dst) in enumerate(zip((w1_in, w2_in), slab(y, z))):
+            push(src, dst, ags.at[w, i], agr.at[w, mine], dev(yy=(y + i) % 4))
+
+    def arrive(yy, zz):
+        for w, ref in enumerate(slab(yy, zz)):
+            wait(ref, agr.at[w, yy * Z + zz])
+
+    def forward(yy, zz, k, to):
+        for w, ref in enumerate(slab(yy, zz)):
+            push(ref, ref, ags.at[w, k], agr.at[w, yy * Z + zz], to)
+
+    def spread_first():
+        for i in range(4):
+            yy = (y + i) % 4
+            if i:
+                arrive(yy, z)
+            forward(yy, z, 4 + i, ahead)
+            forward(yy, z, 4 * half + 4 + i, behind)
+
+    def spread(t):
+        for i in range(4):
+            yy = (y + i) % 4
+            from_behind = (z + Z - turn * t) % Z
+            from_ahead = (z + Z + turn * t) % Z
+            arrive(yy, from_behind)
+            forward(yy, from_behind, 4 + 4 * t + i, ahead)
+            arrive(yy, from_ahead)
+
+            @pl.when(t < half - 1)
+            def _():
+                forward(yy, from_ahead, 4 * half + 4 + 4 * t + i, behind)
+
     loop(0, CHUNKS, first)
 
     def relay(q, recv_kind, k, targets):
@@ -221,20 +265,9 @@
 
     loop(0, CHUNKS + 3, exchange)
 
-    mine = y * Z + z
-
-    def gather(k):
-        to = dev(yy=(y + k // Z) % 4, zz=(z + k % Z) % Z)
-        push(
-            w1_in,
-            W1.at[yl * Z + z, c, :, pl.ds(pl.multiple_of(yh * 256, 256), 256)],
-            ags.at[0, k],
-            agr.at[0, mine],
-            to,
-        )
-        push(w2_in, W2.at[yh, yl * Z + z, c], ags.at[1, k], agr.at[1, mine], to)
-
-    loop(1, 4 * Z, gather)
+    local[4].wait()
+    local[5].wait()
+    spread_first()
 
     def partner_share(k):
         for q, kind in enumerate((3, 5, 6, 7)):
@@ -244,7 +277,7 @@
 
     loop(0, CHUNKS, partner_share)
     wait(gains.at[other], gsem.at[1])
-    for copy in local:
+    for copy in local[:4] + local[6:]:
         copy.wait()
 
     def encode(m):
@@ -282,18 +315,17 @@
         def _():
             push(outbox.at[m], feat, fs.at[m], fr, dev(xx=m))
 
+        @pl.when(jnp.logical_and(x < X - 1, m < half - 1))
+        def _():
+            spread(m + 1)
+
     def project():
-        def arrived(k):
-            yy, zz = k // Z, k % Z
-            row = (yy % 2) * Z + zz
-            col = pl.multiple_of((yy // 2) * 256, 256)
-
-            @pl.when(k != mine)
-            def _():
-                wait(W1.at[row, c, :, pl.ds(col, 256)], agr.at[0, k])
-                wait(W2.at[yy // 2, row, c], agr.at[1, k])
-
-        loop(0, 4 * Z, arrived)
+        @pl.when(x == X - 1)
+        def _():
+            loop(1, half, spread)
+
+        for i in range(4):
+            arrive((y + i) % 4, (z + half) % Z)
         push(W1.at[:, c], W1.at[:, c], pxs.at[0], pxr.at[0], partner)
         for h in range(2):
             push(W2.at[h, :, c], W2.at[h, :, c], pxs.at[1 + h], pxr.at[1 + h], partner)
@@ -407,13 +439,17 @@
     for yy in range(4):
         push(PB.at[1 - c, yy], crecv.at[yy], ccs.at[yy], ccr.at[yy], partner)
 
-    half = Z // 2
-
     def cores(yy):
         wait(crecv.at[yy], ccr.at[yy])
         S[yy] = (PB[c, yy].astype(F32) + crecv[yy].astype(F32)).astype(BF16)
-        push(S.at[yy, (z + half) % Z], urecv.at[0, yy], us.at[0, yy], ur.at[0, yy], up)
-        push(S.at[yy, (z + half + 1) % Z], drecv.at[0, yy], ds_.at[0, yy], dr.at[0, yy], down)
+        push(S.at[yy, (z + half) % Z], urecv.at[0, yy], us.at[0, yy], ur.at[0, yy], ahead)
+        push(
+            S.at[yy, (z + Z + turn * (half + 1)) % Z],
+            drecv.at[0, yy],
+            ds_.at[0, yy],
+            dr.at[0, yy],
+            behind,
+        )
 
     loop(0, 4, cores)
 
@@ -421,18 +457,18 @@
         for yy in range(4):
             wait(urecv.at[t, yy], ur.at[t, yy])
             usend[t, yy] = (
-                urecv[t, yy].astype(F32) + S[yy, (z + half - 1 - t) % Z].astype(F32)
+                urecv[t, yy].astype(F32) + S[yy, (z + Z + turn * (half - 1 - t)) % Z].astype(F32)
             ).astype(BF16)
-            push(usend.at[t, yy], urecv.at[t + 1, yy], us.at[t + 1, yy], ur.at[t + 1, yy], up)
+            push(usend.at[t, yy], urecv.at[t + 1, yy], us.at[t + 1, yy], ur.at[t + 1, yy], ahead)
 
             @pl.when(t < half - 2)
             def _():
                 wait(drecv.at[t, yy], dr.at[t, yy])
                 dsend[t, yy] = (
-                    drecv[t, yy].astype(F32) + S[yy, (z + half + 2 + t) % Z].astype(F32)
+                    drecv[t, yy].astype(F32) + S[yy, (z + Z + turn * (half + 2 + t)) % Z].astype(F32)
                 ).astype(BF16)
                 push(
-                    dsend.at[t, yy], drecv.at[t + 1, yy], ds_.at[t + 1, yy], dr.at[t + 1, yy], down
+                    dsend.at[t, yy], drecv.at[t + 1, yy], ds_.at[t + 1, yy], dr.at[t + 1, yy], behind
                 )
 
     loop(0, half - 1, ring)

time: 159 us -> 159 us (level)
  no operation moved by 1% of the time
where the time goes in v2:
time: 159 us
  Pallas kernels  155 us (97%)
  local copies, waits for them, and re-layouts  2.85 us (2%)
    pallas_call x1, Pallas kernels, on_device(): pl.pallas_call(functools.partial(mega, X, Z), out_shape=(jax.ShapeDtypeSt...  155 us

profile of v2, /device:TPU:24, one launch (start us, length us, event | category | flops | bytes accessed | tf_op | source)
XLA Modules:
  0.0 158.9 jit_solution(12005322958227310134)
XLA Ops:
  0.6 155.4 %shard_map.86 = (f32[64,256]{1,0:T(8,128)}, f32[8,1024]{1,0:T(8,128)}) custom-call(bf16[1024,1024]{1,0:T(8,128)(2,1)} %bitcast.6, f32[1,1024]{1,0:T(1,128)} %gain_in.1, bf16[1024,2048]{1,0:T(8,128)(2,1)} %bitcast.4, bf16[2048,1024]{1,0:T(8,128)(2,1)} %bitcast.5, bf16[128,2048]{1,0:T(8,128)(2,1)} %bitcast.7, bf16[64,256]{1,0:T(8,128)(2,1)} %w1_in.1, ...), custom_call_target="tpu_custom_call" | custom-call | tf_op jit(solution)/shard_map/pallas_call | solution.py:625
  156.1 1.5 copy.11
  157.5 1.4 copy.12

commit v3 on v2

--- a/solution.py
+++ b/solution.py
@@ -153,8 +153,11 @@
     greet(partner)
     for i in range(1, X):
         greet(dev(xx=(x + i) % X))
-    loop(1, 4 * Z, lambda k: greet(dev(yy=(y + k // Z) % 4, zz=(z + k % Z) % Z)))
-    pl.semaphore_wait(barrier, 1 + (X - 1) + (4 * Z - 1))
+    for i in range(1, 4):
+        greet(dev(yy=(y + i) % 4))
+    greet(up)
+    greet(down)
+    pl.semaphore_wait(barrier, 1 + (X - 1) + 3 + 2)
 
     for i in range(1, X):
         push(hid_in, hid.at[x], hs.at[i], hr.at[x], dev(xx=(x + i) % X))
@@ -414,6 +417,29 @@
         preferred_element_type=F32,
     ).reshape(2, 2, Z, 2, 8, D)
     gpv = gp[...].reshape(tokens, gp.shape[2])
+    for cc in range(2):
+        for yy in range(4):
+            for zz in range(Z):
+                blk = g2[yy // 2, yy % 2, zz, cc]
+                PB[cc, yy, zz, 64:96, :] = jnp.concatenate(
+                    [blk[:, k * 256 : k * 256 + 256] for k in range(4)], axis=0
+                ).astype(BF16)
+
+    def swap(yy):
+        push(PB.at[1 - c, yy], crecv.at[yy], ccs.at[yy], ccr.at[yy], partner)
+
+    def cores(yy):
+        wait(crecv.at[yy], ccr.at[yy])
+        S[yy] = (PB[c, yy].astype(F32) + crecv[yy].astype(F32)).astype(BF16)
+        push(S.at[yy, (z + half) % Z], urecv.at[0, yy], us.at[0, yy], ur.at[0, yy], ahead)
+        push(
+            S.at[yy, (z + Z + turn * (half + 1)) % Z],
+            drecv.at[0, yy],
+            ds_.at[0, yy],
+            dr.at[0, yy],
+            behind,
+        )
+
     span = Z // 2 * 2 * 64
     for q in range(4):
         g1 = lax.dot_general(
@@ -428,33 +454,15 @@
                 PB[cc, yh2 * 2 + yl2, z2 : z2 + Z // 2, 0:64, :] = g1[
                     :, cc, :, yh2 * 256 : yh2 * 256 + 256
                 ].astype(BF16)
-    for cc in range(2):
-        for yy in range(4):
-            for zz in range(Z):
-                blk = g2[yy // 2, yy % 2, zz, cc]
-                PB[cc, yy, zz, 64:96, :] = jnp.concatenate(
-                    [blk[:, k * 256 : k * 256 + 256] for k in range(4)], axis=0
-                ).astype(BF16)
-
-    for yy in range(4):
-        push(PB.at[1 - c, yy], crecv.at[yy], ccs.at[yy], ccr.at[yy], partner)
-
-    def cores(yy):
-        wait(crecv.at[yy], ccr.at[yy])
-        S[yy] = (PB[c, yy].astype(F32) + crecv[yy].astype(F32)).astype(BF16)
-        push(S.at[yy, (z + half) % Z], urecv.at[0, yy], us.at[0, yy], ur.at[0, yy], ahead)
-        push(
-            S.at[yy, (z + Z + turn * (half + 1)) % Z],
-            drecv.at[0, yy],
-            ds_.at[0, yy],
-            dr.at[0, yy],
-            behind,
-        )
-
-    loop(0, 4, cores)
+        if q % 2:
+            swap(yl2)
+            swap(2 + yl2)
+        if q == 2:
+            loop(0, 2, lambda i: cores(2 * i))
+    loop(0, 2, lambda i: cores(2 * i + 1))
 
     def ring(t):
-        for yy in range(4):
+        for yy in (0, 2, 1, 3):
             wait(urecv.at[t, yy], ur.at[t, yy])
             usend[t, yy] = (
                 urecv[t, yy].astype(F32) + S[yy, (z + Z + turn * (half - 1 - t)) % Z].astype(F32)
@@ -628,7 +636,7 @@
                 jax.ShapeDtypeStruct((64, 256), F32),
                 jax.ShapeDtypeStruct((8, D), F32),
             ),
-            in_specs=[any_, vmem, any_, any_, any_, vmem, vmem],
+            in_specs=[any_] * 7,
             out_specs=(vmem, vmem),
             scratch_shapes=scratch,
             compiler_params=pltpu.CompilerParams(

time: 159 us -> 158 us (level)
  no operation moved by 1% of the time
where the time goes in v3:
time: 158 us; the launch traced here: 157 us
  Pallas kernels  154 us (97%)
  local copies, waits for them, and re-layouts  2.85 us (2%)
    pallas_call x1, Pallas kernels, on_device(): pl.pallas_call(functools.partial(mega, X, Z), out_shape=(jax.ShapeDtypeSt...  154 us

profile of v3, /device:TPU:24, one launch (start us, length us, event | category | flops | bytes accessed | tf_op | source)
XLA Modules:
  0.0 157.5 jit_solution(11513819429047088624)
XLA Ops:
  0.6 154.0 %shard_map.86 = (f32[64,256]{1,0:T(8,128)}, f32[8,1024]{1,0:T(8,128)}) custom-call(bf16[1024,1024]{1,0:T(8,128)(2,1)} %bitcast.6, f32[1,1024]{1,0:T(1,128)} %gain_in.1, bf16[1024,2048]{1,0:T(8,128)(2,1)} %bitcast.4, bf16[2048,1024]{1,0:T(8,128)(2,1)} %bitcast.5, bf16[128,2048]{1,0:T(8,128)(2,1)} %bitcast.7, bf16[64,256]{1,0:T(8,128)(2,1)} %w1_in.1, ...), custom_call_target="tpu_custom_call" | custom-call | tf_op jit(solution)/shard_map/pallas_call | solution.py:633
  154.6 1.5 copy.11
  156.1 1.4 copy.12

commit v4 on v3

--- a/solution.py
+++ b/solution.py
@@ -11,7 +11,7 @@
 GELU_C = 0.7978845608
 F32 = jnp.float32
 BF16 = jnp.bfloat16
-CHUNKS = 8
+CHUNKS = 4
 
 
 def gelu(v):

time: 158 us -> 162 us (1.025)
  Pallas kernels: 154 us -> 158 us
    pallas_call x1, Pallas kernels: 154 us -> 158 us  [on_device(): pl.pallas_call(functools.partial(mega, X, Z), out_shape=(jax.ShapeDtypeSt...]
where the time goes in v4:
time: 162 us
  Pallas kernels  158 us (98%)
  local copies, waits for them, and re-layouts  2.85 us (2%)
    pallas_call x1, Pallas kernels, on_device(): pl.pallas_call(functools.partial(mega, X, Z), out_shape=(jax.ShapeDtypeSt...  158 us

profile of v4, /device:TPU:24, one launch (start us, length us, event | category | flops | bytes accessed | tf_op | source)
XLA Modules:
  0.0 161.5 jit_solution(19949557958720261)
XLA Ops:
  0.6 158.1 %shard_map.86 = (f32[64,256]{1,0:T(8,128)}, f32[8,1024]{1,0:T(8,128)}) custom-call(bf16[1024,1024]{1,0:T(8,128)(2,1)} %bitcast.6, f32[1,1024]{1,0:T(1,128)} %gain_in.1, bf16[1024,2048]{1,0:T(8,128)(2,1)} %bitcast.4, bf16[2048,1024]{1,0:T(8,128)(2,1)} %bitcast.5, bf16[128,2048]{1,0:T(8,128)(2,1)} %bitcast.7, bf16[64,256]{1,0:T(8,128)(2,1)} %w1_in.1, ...), custom_call_target="tpu_custom_call" | custom-call | tf_op jit(solution)/shard_map/pallas_call | solution.py:633
  158.7 1.5 copy.11
  160.2 1.4 copy.12
